TPU v7x, 256 devices: a whole 4x4x8 slice. The times are simulated.
256 devices in a mesh: row: 16 (over x, y), col: 16 (over z, core).
Axes of the slice: x: 4, y: 4, z: 8, core: 2. Of those that a mesh axis runs over, the one named last changes fastest.
Arguments:
- values: bfloat16 [8192, 8192], P('row', 'col'), may hold values from 0.0001296997 to 0.12988281
- tile_mask: int32 [64, 64], P('row', 'col'), may hold values 0 or 1
- keep_mask: int32 [64, 64], P('row', 'col'), may hold values 0 or 1
- thr_index: int32 [8192], P('col'), may hold values from 0 to 9
Outputs:
- expanded: bfloat16 [8192, 8192], P('row', 'col')
All inputs are finite; a program needn't handle non-finite values. No bound on the sum of `tile_mask` or of `keep_mask` on one device may be relied on, other than what follows from the above.
Results may differ from a plain program's by a relative error of at most 0.0004.
Values may be sent and summed in bfloat16 or wider, within the bound.
A program may use at most 64 MiB of HBM per device.

v0:
```python
import jax
import jax.numpy as jnp
from jax import lax
from jax.sharding import Mesh
from jax.sharding import PartitionSpec as P

TB = 128
ROW = ("row_0", "row_1")


def over_axes(x, axes):
    for axis in axes:
        x = lax.psum(x, axis)
    return x


def on_device(values, tile_mask, keep_mask, thr_index):
    row_count, col_count = values.shape
    row_tiles = row_count // TB
    col_tiles = col_count // TB
    matrix = (
        values.reshape(row_tiles, TB, col_tiles, TB)
        * tile_mask[:, None, :, None].astype(jnp.bfloat16)
    ).reshape(row_count, col_count)
    kept_cells = jnp.broadcast_to(
        keep_mask[:, None, :, None].astype(jnp.float32), (row_tiles, TB, col_tiles, TB)
    ).reshape(row_count, col_count)
    order_all = row_count * lax.axis_size(ROW)
    thresholds = 0.125 * thr_index.astype(jnp.float32)
    col_panel = lax.all_gather(matrix, ROW, axis=0, tiled=True)
    product = jnp.dot(
        lax.all_gather(matrix, "col", axis=1, tiled=True),
        col_panel,
        preferred_element_type=jnp.float32,
    )
    outputs = []
    for phase_idx in range(col_tiles):
        lo_col = phase_idx * TB
        part_prod = product[:, lo_col : lo_col + TB]
        col_means = over_axes(jnp.sum(part_prod, axis=0), ROW) / order_all
        pruned = (
            jnp.maximum(part_prod - thresholds[lo_col : lo_col + TB] * col_means, 0.0)
            * kept_cells[:, lo_col : lo_col + TB]
        )
        col_totals = over_axes(jnp.sum(pruned, axis=0), ROW) / order_all
        outputs.append(pruned / jnp.maximum(col_totals, 0.1))
    result = jnp.concatenate(outputs, axis=1)
    return result.astype(jnp.bfloat16)


def solution(mesh):
    finer = Mesh(mesh.devices.reshape(4, 4, mesh.shape["col"]), ("row_0", "row_1", "col"))
    placed = (P(ROW, "col"), P(ROW, "col"), P(ROW, "col"), P("col"))
    return jax.shard_map(
        on_device, mesh=finer, in_specs=placed, out_specs=P(ROW, "col"), check_vma=False
    )
```

profile of v0, /device:TPU:8, one launch (start us, length us, event | category | flops | bytes accessed | tf_op | source)
XLA Modules:
  0.0 198.8 jit_solution(1561034129201004434)
XLA Ops:
  6.5 0.0 all-gather.3.cloned.1.call-start
  6.5 0.7 convert_element_type.12
  7.2 0.2 mul.41
  7.4 1.9 bitcast_multiply_fusion
  9.3 0.0 all-gather.3.cloned.1.call-update
  9.4 0.0 all-gather.5.cloned.1.call-start
  9.4 0.7 all-gather.5.cloned.1.call-update
  10.1 0.7 convert_element_type.14
  10.8 0.2 broadcast_in_dim.2
  11.0 0.1 copy.9
  11.1 0.7 convert_multiply_fusion
  11.8 56.5 %all-gather.3.cloned.1.call-done = bf16[512,8192]{1,0:T(8,128)(2,1)} async-done(((bf16[512,512]{1,0:T(8,128)(2,1)}), bf16[512,8192]{1,0:T(8,128)(2,1)}) %all-gather.3.cloned.1.call-update) | async-done | bytes 8388624 | tf_op jit(solution)/shard_map/all_gather | solution.py:32
  68.2 76.8 %all-gather.5.cloned.1.call-done = bf16[8192,512]{1,0:T(8,128)(2,1)} async-done(((bf16[512,512]{1,0:T(8,128)(2,1)}), bf16[8192,512]{1,0:T(8,128)(2,1)}) %all-gather.5.cloned.1.call-update) | async-done | bytes 8388624 | tf_op jit(solution)/shard_map/all_gather | solution.py:30
  145.0 9.4 %fusion.4 = f32[512,512]{1,0:T(8,128)S(1)} fusion(bf16[512,8192]{1,0:T(8,128)(2,1)} %all-gather.3.cloned.1.call-done, bf16[8192,512]{1,0:T(8,128)(2,1)} %all-gather.5.cloned.1.call-done), kind=kOutput, calls=%fused_computation.28 | convolution fusion | flops 4294967296 | bytes 17825792 | tf_op jit(solution)/shard_map/dot_general | solution.py:31
  154.5 0.1 slice_reduce_fusion.3
  154.6 9.2 %all-reduce.3 = (f32[128]{0:T(128)S(1)}, f32[128]{0:T(128)S(1)}, f32[128]{0:T(128)S(1)}, f32[128]{0:T(128)S(1)}) all-reduce(f32[128]{0:T(128)S(1)} %get-tuple-element.9, f32[128]{0:T(128)S(1)} %get-tuple-element.10, f32[128]{0:T(128)S(1)} %get-tuple-element.11, ...), channel_id=1, replica_groups=mesh['row_0'=4,'row_1'=4,'col'=16] {'row_0'}, use_global_device_ids=true, to_apply=%region_1.0 | all-reduce | flops 512 | bytes 4096 | tf_op jit(solution)/shard_map/psum | solution.py:13
  163.8 9.5 %all-reduce.1 = (f32[128]{0:T(128)S(1)}, f32[128]{0:T(128)S(1)}, f32[128]{0:T(128)S(1)}, f32[128]{0:T(128)S(1)}) all-reduce(f32[128]{0:T(128)S(1)} %get-tuple-element.25, f32[128]{0:T(128)S(1)} %get-tuple-element.26, f32[128]{0:T(128)S(1)} %get-tuple-element.27, ...), channel_id=1, replica_groups=mesh['row_0'=4,'row_1'=4,'col'=16] {'row_1'}, use_global_device_ids=true, to_apply=%region_2.0 | all-reduce | flops 512 | bytes 4096 | tf_op jit(solution)/shard_map/psum | solution.py:13
  173.3 0.2 fusion
  173.5 7.7 %all-reduce.2 = (f32[128]{0:T(128)S(1)}, f32[128]{0:T(128)S(1)}, f32[128]{0:T(128)S(1)}, f32[128]{0:T(128)S(1)}) all-reduce(f32[128]{0:T(128)S(1)} %get-tuple-element.6, f32[128]{0:T(128)S(1)} %get-tuple-element.7, f32[128]{0:T(128)S(1)} %get-tuple-element.8, ...), channel_id=1, replica_groups=mesh['row_0'=4,'row_1'=4,'col'=16] {'row_0'}, use_global_device_ids=true, to_apply=%region_22.0 | all-reduce | flops 512 | bytes 4096 | tf_op jit(solution)/shard_map/psum | solution.py:13
  181.2 9.7 %all-reduce = (f32[128]{0:T(128)S(1)}, f32[128]{0:T(128)S(1)}, f32[128]{0:T(128)S(1)}, f32[128]{0:T(128)S(1)}) all-reduce(f32[128]{0:T(128)S(1)} %get-tuple-element.21, f32[128]{0:T(128)S(1)} %get-tuple-element.22, f32[128]{0:T(128)S(1)} %get-tuple-element.23, ...), channel_id=1, replica_groups=mesh['row_0'=4,'row_1'=4,'col'=16] {'row_1'}, use_global_device_ids=true, to_apply=%region_23.0 | all-reduce | flops 512 | bytes 4096 | tf_op jit(solution)/shard_map/psum | solution.py:13
  191.0 0.2 divide_convert_fusion.3
  191.2 0.9 pad_maximum_fusion
  (3 shorter events, 0.0 us)
Async XLA Ops:
  6.5 61.7 %all-gather.3.cloned.1.call-start = ((), (), s32[]{:S(2)}) async-start(), calls=%async_computation | async-start | bytes 8912896 | tf_op jit(solution)/shard_map/all_gather | solution.py:32
  9.4 135.7 %all-gather.5.cloned.1.call-start = ((), (), s32[]{:S(2)}) async-start(), calls=%async_computation.1 | async-start | bytes 8912896 | tf_op jit(solution)/shard_map/all_gather | solution.py:30
Sparse Core Ops, SparseCore 0:
  9.5 58.7 all-gather.2
  70.7 74.2 all-gather.4
where the time goes:
time: 199 us
  waiting for transfers between devices  134 us (67%)
  blocking collectives  36.2 us (18%)
  between operations  13.4 us (7%)
  matrix products  9.44 us (5%)
  other arithmetic  5.27 us (3%)
    all_gather x1, waiting for transfers between devices, on_device(): col_panel = lax.all_gather(matrix, ROW, axis=0, tiled=True)  76.8 us
    all_gather x1, waiting for transfers between devices, on_device(): lax.all_gather(matrix, 'col', axis=1, tiled=True)  56.5 us
    psum x4, blocking collectives, over_axes(): x = lax.psum(x, axis)  36.2 us
    dot_general x1, matrix products, on_device(): jnp.dot(lax.all_gather(matrix, 'col', axis=1, tiled=True), col_panel, pre...  9.44 us
  transfers between devices with their start and end apart: 2, of which 2 were waited for; matrix products, arithmetic and copies ran while one was open for 1% of the time, Pallas kernels for 0%

commit v1 on v0

v1 whole, which is shorter than its diff:
```python
import functools

import jax
import jax.numpy as jnp
from jax import lax
from jax.experimental import pallas as pl
from jax.experimental.pallas import tpu as pltpu
from jax.sharding import PartitionSpec as P

TB = 128
BLOCK = 512
HALF = BLOCK // 2
QUART = BLOCK // 4
TILES = BLOCK // TB
GROUP = 16
SIDE = 4
DEPTH = 8
ORDER = BLOCK * GROUP
AUG = 16
EVENTS = 13
MESH = pl.DeviceIdType.MESH

UPPER, LOWER = (0, HALF), (HALF, HALF)


def quarter(half, step):
    return (half[0] + (0 if step > 0 else QUART), QUART)


def plane_queue(axis, step):
    def at(along, across):
        return (along, across) if axis == 0 else (across, along)

    first, second = (UPPER, LOWER) if axis == 0 else (LOWER, UPPER)
    return [
        (at(0, 0), first, 0),
        (at(0, 0), second, 0),
        (at(-step, 0), quarter(first, step), 1),
        (at(0, -1), second, 1),
        (at(0, 1), second, 1),
        (at(-step, 0), quarter(second, step), 2),
        (at(0, 2), second, 3),
        (at(-step, -1), quarter(second, step), 5),
        (at(-step, 1), quarter(second, step), 7),
        (at(-step, 2), quarter(second, step), 9),
    ]


PLANE_ARRIVAL = [1, 2, 3, 5, 7, 8, 9, 10, 11, 12]


def depth_queue(step):
    first, second = (UPPER, LOWER) if step > 0 else (LOWER, UPPER)
    return [
        (0, first, 0),
        (0, second, 0),
        (-step, first, 1),
        (-step, second, 2),
        (-2 * step, first, 4),
        (-2 * step, second, 6),
        (-3 * step, first, 8),
    ]


DEPTH_ARRIVAL = [1, 2, 4, 6, 8, 9, 11]


def wrap(value, size):
    return lax.rem(value + size, size)


def kernel(
    values_ref, tile_hbm, keep_hbm, thr_hbm, pruned_ref, total_ref, tile_ref, keep_ref, thr_ref,
    rows_buf, cols_buf, acc, own, part_buf, sum_buf, tot_buf,
    in_sem, send_sem, recv_sem, part_send, part_recv, sum_send, sum_recv, tot_send, tot_recv,
):
    me_row, me_col = lax.axis_index("row"), lax.axis_index("col")
    x, y = lax.div(me_row, SIDE), lax.rem(me_row, SIDE)
    z, core = lax.div(me_col, 2), lax.rem(me_col, 2)

    def row_of(dx, dy):
        return wrap(x + dx, SIDE) * SIDE + wrap(y + dy, SIDE)

    def col_of(dz, other=0):
        return wrap(z + dz, DEPTH) * 2 + (1 - core if other else core)

    barrier = pltpu.get_barrier_semaphore()

    def greet(i, carry):
        pl.semaphore_signal(barrier, inc=1, device_id=(lax.rem(me_row + i, GROUP), me_col), device_id_type=MESH)
        pl.semaphore_signal(barrier, inc=1, device_id=(me_row, lax.rem(me_col + i, GROUP)), device_id_type=MESH)
        return carry

    lax.fori_loop(1, GROUP, greet, 0)
    loads = [
        pltpu.make_async_copy(out, into, in_sem.at[i])
        for i, (out, into) in enumerate(
            ((values_ref, own), (tile_hbm, tile_ref), (keep_hbm, keep_ref), (thr_hbm, thr_ref))
        )
    ]
    for load in loads:
        load.start()

    copies = []

    def copy_of(buf, slot, rows, number, target):
        part = buf.at[slot, pl.ds(*rows), :]
        return pltpu.make_async_remote_copy(
            src_ref=part, dst_ref=part, send_sem=send_sem.at[number], recv_sem=recv_sem.at[number],
            device_id=target, device_id_type=MESH,
        )

    def add(buf, sent_slot, got_slot, rows, target, leaves, arrives):
        number = len(copies)
        copies.append((
            leaves, arrives,
            copy_of(buf, sent_slot, rows, number, target),
            copy_of(buf, got_slot, rows, number, target),
        ))

    for place in range(10):
        for axis in (0, 1):
            for step in (1, -1):
                (dx, dy), rows, leaves = plane_queue(axis, step)[place]
                sx, sy = (step, 0) if axis == 0 else (0, step)
                add(
                    cols_buf, row_of(dx, dy), row_of(dx - sx, dy - sy), rows,
                    (row_of(sx, sy), me_col), leaves, PLANE_ARRIVAL[place],
                )
        if place < 7:
            for step in (1, -1):
                dz, rows, leaves = depth_queue(step)[place]
                add(
                    rows_buf, col_of(dz), col_of(dz - step), rows,
                    (me_row, col_of(step)), leaves, DEPTH_ARRIVAL[place],
                )
    partner = (me_row, col_of(0, 1))
    for half in (UPPER, LOWER):
        add(rows_buf, col_of(0), col_of(0, 1), half, partner, 0, 1)
    for place in range(7):
        for step in (1, -1):
            dz, rows, _ = depth_queue(step)[place]
            add(
                rows_buf, col_of(dz - step), col_of(dz - step, 1), rows, partner,
                DEPTH_ARRIVAL[place], DEPTH_ARRIVAL[place] + 1,
            )

    def send(event):
        for leaves, _, out, _ in copies:
            if leaves == event:
                out.start()

    def receive(event):
        for _, arrives, _, into in copies:
            if arrives == event:
                into.wait_recv()

    def share(buf, sends, recvs, along_row):
        def out(i):
            if along_row:
                target, slot = (lax.rem(me_row + i, GROUP), me_col), me_row
            else:
                target, slot = (me_row, lax.rem(me_col + i, GROUP)), me_col
            return pltpu.make_async_remote_copy(
                src_ref=buf.at[slot], dst_ref=buf.at[slot], send_sem=sends.at[i], recv_sem=recvs.at[i],
                device_id=target, device_id_type=MESH,
            )

        def into(i):
            if along_row:
                target, slot = (lax.rem(me_row + i, GROUP), me_col), lax.rem(me_row + GROUP - i, GROUP)
            else:
                target, slot = (me_row, lax.rem(me_col + i, GROUP)), lax.rem(me_col + GROUP - i, GROUP)
            return pltpu.make_async_remote_copy(
                src_ref=buf.at[slot], dst_ref=buf.at[slot], send_sem=sends.at[i], recv_sem=recvs.at[i],
                device_id=target, device_id_type=MESH,
            )

        def start(i, carry):
            out(i).start()
            return carry

        def arrive(i, carry):
            into(i).wait_recv()
            return carry

        def finish(i, carry):
            out(i).wait_send()
            return carry

        return tuple(functools.partial(lax.fori_loop, 1, GROUP, f, 0) for f in (start, arrive, finish))

    part_start, part_arrive, part_finish = share(part_buf, part_send, part_recv, True)
    sum_start, sum_arrive, sum_finish = share(sum_buf, sum_send, sum_recv, False)
    tot_start, tot_arrive, tot_finish = share(tot_buf, tot_send, tot_recv, True)

    for load in loads:
        load.wait()
    for j in range(TILES):
        cols = slice(j * TB, (j + 1) * TB)
        part = jnp.zeros((1, TB), jnp.float32)
        for i in range(TILES):
            rows = slice(i * TB, (i + 1) * TB)
            tile = own[rows, cols].astype(jnp.float32) * tile_ref[i, j].astype(jnp.float32)
            part += jnp.sum(tile, axis=0, keepdims=True)
            rows_buf[me_col, rows, cols] = tile.astype(jnp.bfloat16)
            cols_buf[me_row, rows, cols] = tile.astype(jnp.bfloat16)
        part_buf[me_row, :, cols] = part
    acc[...] = jnp.zeros_like(acc)

    pl.semaphore_wait(barrier, 2 * (GROUP - 1))
    part_start()
    send(0)

    part_arrive()
    sums = part_buf[0]
    for i in range(1, GROUP):
        sums += part_buf[i]
    sum_buf[me_col] = sums
    part_finish()
    receive(1)
    sum_start()
    send(1)

    def multiply(stage):
        def one(k, carry):
            dx = wrap(lax.div(k, SIDE) - x, SIDE)
            dy = wrap(lax.rem(k, SIDE) - y, SIDE)
            dz = wrap(lax.div(k, 2) - z, DEPTH)

            def far(d):
                return lax.div(d * (SIDE - d), 4)

            def off(d):
                return lax.div(d + 3, 4)

            n = (far(dx) + far(dy)) * off(dx) * off(dy)
            by_plane = n + lax.div(n + 1, 2)
            reach = dz * (DEPTH - dz)
            by_depth = lax.div(reach, 15) + 2 * lax.div(reach, 16)

            @pl.when(jnp.maximum(by_plane, by_depth) == stage)
            def _():
                acc[...] += jnp.dot(rows_buf[k], cols_buf[k], preferred_element_type=jnp.float32)

            return carry

        lax.fori_loop(0, GROUP, one, 0)

    for event in range(2, EVENTS):
        receive(event)
        send(event)
        if event == 8:
            sum_arrive()

            def augment(k, carry):
                s = sum_buf[k]
                high = s.astype(jnp.bfloat16).astype(jnp.float32)
                rest = s - high
                mid = rest.astype(jnp.bfloat16).astype(jnp.float32)
                low = rest - mid
                index = lax.broadcasted_iota(jnp.int32, (AUG, BLOCK), 0)
                rows = jnp.where(index == 0, high, jnp.where(index == 1, mid, jnp.where(index == 2, low, 0.0)))
                rows_buf[k, BLOCK:, :] = rows.astype(jnp.bfloat16)
                return carry

            lax.fori_loop(0, GROUP, augment, 0)
        stage = {8: 0, 10: 1, 11: 2, 12: 3}.get(event)
        if stage is not None:
            multiply(stage)

    means = (acc[BLOCK : BLOCK + 1, :] + acc[BLOCK + 1 : BLOCK + 2, :] + acc[BLOCK + 2 : BLOCK + 3, :]) / ORDER
    cut = 0.125 * thr_ref[...].astype(jnp.float32) * means
    for j in range(TILES):
        cols = slice(j * TB, (j + 1) * TB)
        part = jnp.zeros((1, TB), jnp.float32)
        for i in range(TILES):
            rows = slice(i * TB, (i + 1) * TB)
            tile = jnp.maximum(acc[rows, cols] - cut[:, cols], 0.0) * keep_ref[i, j].astype(jnp.float32)
            pruned_ref[rows, cols] = tile
            part += jnp.sum(tile, axis=0, keepdims=True)
        tot_buf[me_row, :, cols] = part
    for _, _, out, _ in copies:
        out.wait_send()
    tot_start()
    sum_finish()
    tot_arrive()
    totals = tot_buf[0]
    for i in range(1, GROUP):
        totals += tot_buf[i]
    total_ref[...] = totals
    tot_finish()


def n_copies():
    return 40 + 14 + 16


def on_device(values, tile_mask, keep_mask, thr_index):
    vmem = pl.BlockSpec(memory_space=pltpu.VMEM)
    hbm = pl.BlockSpec(memory_space=pltpu.HBM)
    dma = pltpu.SemaphoreType.DMA
    pruned, totals = pl.pallas_call(
        kernel,
        out_shape=(
            jax.ShapeDtypeStruct((BLOCK, BLOCK), jnp.float32),
            jax.ShapeDtypeStruct((1, BLOCK), jnp.float32),
        ),
        in_specs=[hbm, hbm, hbm, hbm],
        out_specs=(vmem, vmem),
        scratch_shapes=[
            pltpu.SMEM((TILES, TILES), jnp.int32),
            pltpu.SMEM((TILES, TILES), jnp.int32),
            pltpu.VMEM((1, BLOCK), jnp.int32),
            pltpu.VMEM((GROUP, BLOCK + AUG, BLOCK), jnp.bfloat16),
            pltpu.VMEM((GROUP, BLOCK, BLOCK), jnp.bfloat16),
            pltpu.VMEM((BLOCK + AUG, BLOCK), jnp.float32),
            pltpu.VMEM((BLOCK, BLOCK), jnp.bfloat16),
            pltpu.VMEM((GROUP, 1, BLOCK), jnp.float32),
            pltpu.VMEM((GROUP, 1, BLOCK), jnp.float32),
            pltpu.VMEM((GROUP, 1, BLOCK), jnp.float32),
            dma((4,)), dma((n_copies(),)), dma((n_copies(),)),
            dma((GROUP,)), dma((GROUP,)), dma((GROUP,)), dma((GROUP,)), dma((GROUP,)), dma((GROUP,)),
        ],
        compiler_params=pltpu.CompilerParams(
            collective_id=0, has_side_effects=True, vmem_limit_bytes=40 * 1024 * 1024
        ),
        cost_estimate=pl.CostEstimate(
            flops=2 * BLOCK * BLOCK * ORDER, bytes_accessed=2 * 1024 * 1024, transcendentals=0
        ),
        name="expand",
    )(*(pltpu.with_memory_space_constraint(a, pltpu.HBM) for a in (values, tile_mask, keep_mask, thr_index.reshape(1, BLOCK))))
    return (pruned / jnp.maximum(totals / ORDER, 0.1)).astype(jnp.bfloat16)


def solution(mesh):
    return jax.shard_map(
        on_device,
        mesh=mesh,
        in_specs=(P("row", "col"), P("row", "col"), P("row", "col"), P("col")),
        out_specs=P("row", "col"),
        check_vma=False,
    )
```

time: 199 us -> 64.6 us (0.32)
  waiting for transfers between devices: 134 us -> 0 us
  Pallas kernels: 0 us -> 62.9 us
  blocking collectives: 36.2 us -> 0 us
  between operations: 13.4 us -> 0.02 us
  matrix products: 9.44 us -> 0 us
  other arithmetic: 5.27 us -> 0.92 us
    all_gather x2 -> x0, waiting for transfers between devices: 133 us -> none  [the longest x1 76.8 us: on_device(): col_panel = lax.all_gather(matrix, ROW, axis=0, tiled=True)]
    pallas_call x0 -> x1, Pallas kernels: none -> 62.9 us  [on_device(): pl.pallas_call(kernel, out_shape=(jax.ShapeDtypeStruct((BLOCK, BLOCK), jn...]
    psum x4 -> x0, blocking collectives: 36.2 us -> none  [over_axes(): x = lax.psum(x, axis)]
    dot_general x1 -> x0, matrix products: 9.44 us -> none  [on_device(): jnp.dot(lax.all_gather(matrix, 'col', axis=1, tiled=True), col_panel, pre...]
    mul x3 -> x0, other arithmetic: 2.6 us -> none  [the longest x1 1.91 us: on_device(): values.reshape(row_tiles, TB, col_tiles, TB)]
  transfers between devices with their start and end apart: 2 -> 0, of which waited for: 2 -> 0; matrix products, arithmetic and copies ran while one was open for 1% -> 0% of each run, Pallas kernels for 0% -> 0%
where the time goes in v1:
time: 64.6 us; the launch traced here: 63.8 us
  Pallas kernels  62.9 us (97%)
  other arithmetic  0.92 us (1%)
    pallas_call x1, Pallas kernels, on_device(): pl.pallas_call(kernel, out_shape=(jax.ShapeDtypeStruct((BLOCK, BLOCK), jn...  62.9 us

profile of v1, /device:TPU:8, one launch (start us, length us, event | category | flops | bytes accessed | tf_op | source)
XLA Modules:
  0.0 63.8 jit_solution(6905362571435875981)
XLA Ops:
  0.0 62.9 %expand.1 = (f32[512,512]{1,0:T(8,128)S(1)}, f32[1,512]{1,0:T(1,128)S(1)}) custom-call(bf16[512,512]{1,0:T(8,128)(2,1)} %values_ref.1, s32[4,4]{1,0:T(4,128)} %tile_hbm.1, s32[4,4]{1,0:T(4,128)} %keep_hbm.1, s32[1,512]{1,0:T(1,128)} %bitcast.3), custom_call_target="tpu_custom_call" | custom-call | flops 4294967296 | bytes 2097152 | tf_op jit(solution)/shard_map/expand/pallas_call | solution.py:303
  62.9 0.9 %divide_convert_fusion = bf16[512,512]{1,0:T(8,128)(2,1)} fusion(f32[512,512]{1,0:T(8,128)S(1)} %get-tuple-element.7, f32[512]{0:T(512)S(1)} %bitcast.2), kind=kLoop, calls=%fused_computation | loop fusion | flops 524288 | bytes 1574912 | tf_op jit(solution)/shard_map/convert_element_type | solution.py:333
  (1 shorter events, 0.0 us)

commit v2 on v1

--- a/solution.py
+++ b/solution.py
@@ -17,7 +17,7 @@
 DEPTH = 8
 ORDER = BLOCK * GROUP
 AUG = 16
-EVENTS = 13
+ROUNDS = 4
 MESH = pl.DeviceIdType.MESH
 
 UPPER, LOWER = (0, HALF), (HALF, HALF)
@@ -33,36 +33,34 @@
 
     first, second = (UPPER, LOWER) if axis == 0 else (LOWER, UPPER)
     return [
-        (at(0, 0), first, 0),
-        (at(0, 0), second, 0),
-        (at(-step, 0), quarter(first, step), 1),
-        (at(0, -1), second, 1),
-        (at(0, 1), second, 1),
-        (at(-step, 0), quarter(second, step), 2),
-        (at(0, 2), second, 3),
-        (at(-step, -1), quarter(second, step), 5),
-        (at(-step, 1), quarter(second, step), 7),
-        (at(-step, 2), quarter(second, step), 9),
+        (at(0, 0), first, 0, 2),
+        (at(0, 0), second, 0, 4),
+        (at(-step, 0), quarter(first, step), 2, 5),
+        (at(0, -1), second, 2, 7),
+        (at(0, 1), second, 2, 9),
+        (at(-step, 0), quarter(second, step), 4, 10),
+        (at(0, 2), second, 5, 12),
+        (at(-step, -1), quarter(second, step), 7, 13),
+        (at(-step, 1), quarter(second, step), 9, 14),
+        (at(-step, 2), quarter(second, step), 12, 15),
     ]
-
-
-PLANE_ARRIVAL = [1, 2, 3, 5, 7, 8, 9, 10, 11, 12]
 
 
 def depth_queue(step):
     first, second = (UPPER, LOWER) if step > 0 else (LOWER, UPPER)
     return [
-        (0, first, 0),
-        (0, second, 0),
-        (-step, first, 1),
-        (-step, second, 2),
-        (-2 * step, first, 4),
-        (-2 * step, second, 6),
-        (-3 * step, first, 8),
+        (0, first, 0, 2.1, 9.2),
+        (0, second, 0, 4.1, 9.2),
+        (-step, first, 2.1, 6.1, 9.2),
+        (-step, second, 4.1, 8.1, 9.2),
+        (-2 * step, first, 6.1, 10.1, 13.2),
+        (-2 * step, second, 8.1, 12.1, 13.2),
+        (-3 * step, quarter(first, 1), 10.1, 13.1, 15.2),
+        (-3 * step, quarter(first, -1), 10.1, 14.1, 15.2),
     ]
 
 
-DEPTH_ARRIVAL = [1, 2, 4, 6, 8, 9, 11]
+STAGE_AFTER = {9.2: 0, 10.1: 1, 12.1: 2, 13.2: 3, 14.1: 4, 15: 5, 15.2: 6}
 
 
 def wrap(value, size):
@@ -72,7 +70,7 @@
 def kernel(
     values_ref, tile_hbm, keep_hbm, thr_hbm, pruned_ref, total_ref, tile_ref, keep_ref, thr_ref,
     rows_buf, cols_buf, acc, own, part_buf, sum_buf, tot_buf,
-    in_sem, send_sem, recv_sem, part_send, part_recv, sum_send, sum_recv, tot_send, tot_recv,
+    in_sem, send_sem, recv_sem, part_send, part_recv, sum_send, sum_recv, tot_send, tot_recv, ready_sem, round_sem,
 ):
     me_row, me_col = lax.axis_index("row"), lax.axis_index("col")
     x, y = lax.div(me_row, SIDE), lax.rem(me_row, SIDE)
@@ -84,14 +82,6 @@
     def col_of(dz, other=0):
         return wrap(z + dz, DEPTH) * 2 + (1 - core if other else core)
 
-    barrier = pltpu.get_barrier_semaphore()
-
-    def greet(i, carry):
-        pl.semaphore_signal(barrier, inc=1, device_id=(lax.rem(me_row + i, GROUP), me_col), device_id_type=MESH)
-        pl.semaphore_signal(barrier, inc=1, device_id=(me_row, lax.rem(me_col + i, GROUP)), device_id_type=MESH)
-        return carry
-
-    lax.fori_loop(1, GROUP, greet, 0)
     loads = [
         pltpu.make_async_copy(out, into, in_sem.at[i])
         for i, (out, into) in enumerate(
@@ -101,6 +91,26 @@
     for load in loads:
         load.start()
 
+    links = []
+    for axis in (0, 1):
+        for step in (1, -1):
+            dx, dy = (step, 0) if axis == 0 else (0, step)
+            mine = x if axis == 0 else y
+            links.append(((row_of(dx, dy), me_col), wrap(mine + step, SIDE), mine))
+    for step in (1, -1):
+        links.append(((me_row, col_of(step)), wrap(z + step, DEPTH), z))
+    partner = (me_row, col_of(0, 1))
+
+    barrier = pltpu.get_barrier_semaphore()
+    pl.semaphore_signal(barrier, inc=1, device_id=partner, device_id_type=MESH)
+    lower = 1
+    for neighbour, theirs, mine in links:
+        lower += (theirs < mine).astype(jnp.int32)
+
+        @pl.when(theirs > mine)
+        def _(neighbour=neighbour):
+            pl.semaphore_signal(barrier, inc=1, device_id=neighbour, device_id_type=MESH)
+
     copies = []
 
     def copy_of(buf, slot, rows, number, target):
@@ -110,10 +120,10 @@
             device_id=target, device_id_type=MESH,
         )
 
-    def add(buf, sent_slot, got_slot, rows, target, leaves, arrives):
+    def add(buf, sent_slot, got_slot, rows, target, leaves, arrives, link=None):
         number = len(copies)
         copies.append((
-            leaves, arrives,
+            leaves, arrives, link,
             copy_of(buf, sent_slot, rows, number, target),
             copy_of(buf, got_slot, rows, number, target),
         ))
@@ -121,39 +131,40 @@
     for place in range(10):
         for axis in (0, 1):
             for step in (1, -1):
-                (dx, dy), rows, leaves = plane_queue(axis, step)[place]
+                (dx, dy), rows, leaves, arrives = plane_queue(axis, step)[place]
                 sx, sy = (step, 0) if axis == 0 else (0, step)
                 add(
                     cols_buf, row_of(dx, dy), row_of(dx - sx, dy - sy), rows,
-                    (row_of(sx, sy), me_col), leaves, PLANE_ARRIVAL[place],
+                    (row_of(sx, sy), me_col), leaves, arrives, 2 * axis + (step < 0),
                 )
-        if place < 7:
+        if place < 8:
             for step in (1, -1):
-                dz, rows, leaves = depth_queue(step)[place]
+                dz, rows, leaves, arrives, _ = depth_queue(step)[place]
                 add(
                     rows_buf, col_of(dz), col_of(dz - step), rows,
-                    (me_row, col_of(step)), leaves, DEPTH_ARRIVAL[place],
+                    (me_row, col_of(step)), leaves, arrives, 4 + (step < 0),
                 )
-    partner = (me_row, col_of(0, 1))
     for half in (UPPER, LOWER):
-        add(rows_buf, col_of(0), col_of(0, 1), half, partner, 0, 1)
-    for place in range(7):
+        add(rows_buf, col_of(0), col_of(0, 1), half, partner, 0, 9.2)
+    for place in range(8):
         for step in (1, -1):
-            dz, rows, _ = depth_queue(step)[place]
-            add(
-                rows_buf, col_of(dz - step), col_of(dz - step, 1), rows, partner,
-                DEPTH_ARRIVAL[place], DEPTH_ARRIVAL[place] + 1,
-            )
-
-    def send(event):
-        for leaves, _, out, _ in copies:
-            if leaves == event:
+            dz, rows, _, arrives, other = depth_queue(step)[place]
+            add(rows_buf, col_of(dz - step), col_of(dz - step, 1), rows, partner, arrives, other)
+
+    def send(event, link=None):
+        for leaves, _, on, out, _ in copies:
+            if leaves == event and (event > 0 or on == link):
                 out.start()
 
     def receive(event):
-        for _, arrives, _, into in copies:
+        for _, arrives, _, _, into in copies:
             if arrives == event:
                 into.wait_recv()
+
+    def spread(number):
+        for neighbour in [partner] + [link[0] for link in links]:
+            pl.semaphore_signal(round_sem.at[number], inc=1, device_id=neighbour, device_id_type=MESH)
+        pl.semaphore_wait(round_sem.at[number], len(links) + 1)
 
     def share(buf, sends, recvs, along_row):
         def out(i):
@@ -193,6 +204,13 @@
     part_start, part_arrive, part_finish = share(part_buf, part_send, part_recv, True)
     sum_start, sum_arrive, sum_finish = share(sum_buf, sum_send, sum_recv, False)
     tot_start, tot_arrive, tot_finish = share(tot_buf, tot_send, tot_recv, True)
+
+    pl.semaphore_wait(barrier, lower)
+    for number, (neighbour, theirs, mine) in enumerate(links):
+
+        @pl.when(theirs < mine)
+        def _(neighbour=neighbour, number=number):
+            pl.semaphore_signal(ready_sem.at[number ^ 1], inc=1, device_id=neighbour, device_id_type=MESH)
 
     for load in loads:
         load.wait()
@@ -208,19 +226,18 @@
         part_buf[me_row, :, cols] = part
     acc[...] = jnp.zeros_like(acc)
 
-    pl.semaphore_wait(barrier, 2 * (GROUP - 1))
+    send(0)
+    for number, (_, theirs, mine) in enumerate(links):
+
+        @pl.when(theirs > mine)
+        def _(number=number):
+            pl.semaphore_wait(ready_sem.at[number], 1)
+
+        send(0, number)
+
+    for number in range(ROUNDS - 1):
+        spread(number)
     part_start()
-    send(0)
-
-    part_arrive()
-    sums = part_buf[0]
-    for i in range(1, GROUP):
-        sums += part_buf[i]
-    sum_buf[me_col] = sums
-    part_finish()
-    receive(1)
-    sum_start()
-    send(1)
 
     def multiply(stage):
         def one(k, carry):
@@ -234,10 +251,11 @@
             def off(d):
                 return lax.div(d + 3, 4)
 
-            n = (far(dx) + far(dy)) * off(dx) * off(dy)
-            by_plane = n + lax.div(n + 1, 2)
+            n, both = far(dx) + far(dy), off(dx) * off(dy)
+            slow = lax.rem(k + core, 2)
+            by_plane = n * (2 - n) * (1 - both + both * lax.div(11 - dx - dy, 2)) + 5 * lax.div(n * (n - 1), 2)
             reach = dz * (DEPTH - dz)
-            by_depth = lax.div(reach, 15) + 2 * lax.div(reach, 16)
+            by_depth = lax.div(reach, 15) * (2 + slow) + lax.div(reach, 16) * (2 + slow)
 
             @pl.when(jnp.maximum(by_plane, by_depth) == stage)
             def _():
@@ -247,10 +265,20 @@
 
         lax.fori_loop(0, GROUP, one, 0)
 
-    for event in range(2, EVENTS):
+    for event in sorted({arrives for _, arrives, *_ in copies}):
         receive(event)
         send(event)
-        if event == 8:
+        if event == 2.1:
+            spread(ROUNDS - 1)
+        if event == 4.1:
+            part_arrive()
+            sums = part_buf[0]
+            for i in range(1, GROUP):
+                sums += part_buf[i]
+            sum_buf[me_col] = sums
+            part_finish()
+            sum_start()
+        if event == 9.2:
             sum_arrive()
 
             def augment(k, carry):
@@ -265,9 +293,8 @@
                 return carry
 
             lax.fori_loop(0, GROUP, augment, 0)
-        stage = {8: 0, 10: 1, 11: 2, 12: 3}.get(event)
-        if stage is not None:
-            multiply(stage)
+        if event in STAGE_AFTER:
+            multiply(STAGE_AFTER[event])
 
     means = (acc[BLOCK : BLOCK + 1, :] + acc[BLOCK + 1 : BLOCK + 2, :] + acc[BLOCK + 2 : BLOCK + 3, :]) / ORDER
     cut = 0.125 * thr_ref[...].astype(jnp.float32) * means
@@ -280,10 +307,10 @@
             pruned_ref[rows, cols] = tile
             part += jnp.sum(tile, axis=0, keepdims=True)
         tot_buf[me_row, :, cols] = part
-    for _, _, out, _ in copies:
+    sum_finish()
+    tot_start()
+    for _, _, _, out, _ in copies:
         out.wait_send()
-    tot_start()
-    sum_finish()
     tot_arrive()
     totals = tot_buf[0]
     for i in range(1, GROUP):
@@ -293,7 +320,7 @@
 
 
 def n_copies():
-    return 40 + 14 + 16
+    return 40 + 16 + 2 + 16
 
 
 def on_device(values, tile_mask, keep_mask, thr_index):
@@ -321,6 +348,7 @@
             pltpu.VMEM((GROUP, 1, BLOCK), jnp.float32),
             dma((4,)), dma((n_copies(),)), dma((n_copies(),)),
             dma((GROUP,)), dma((GROUP,)), dma((GROUP,)), dma((GROUP,)), dma((GROUP,)), dma((GROUP,)),
+            pltpu.SemaphoreType.REGULAR((6,)), pltpu.SemaphoreType.REGULAR((ROUNDS,)),
         ],
         compiler_params=pltpu.CompilerParams(
             collective_id=0, has_side_effects=True, vmem_limit_bytes=40 * 1024 * 1024

time: 64.6 us -> 63.8 us (0.988)
  no operation moved by 1% of the time
where the time goes in v2:
time: 63.8 us; the launch traced here: 63.5 us
  Pallas kernels  62.6 us (98%)
  other arithmetic  0.92 us (1%)
    pallas_call x1, Pallas kernels, on_device(): pl.pallas_call(kernel, out_shape=(jax.ShapeDtypeStruct((BLOCK, BLOCK), jn...  62.6 us

profile of v2, /device:TPU:8, one launch (start us, length us, event | category | flops | bytes accessed | tf_op | source)
XLA Modules:
  0.0 63.5 jit_solution(196424306118824486)
XLA Ops:
  0.0 62.6 %expand.1 = (f32[512,512]{1,0:T(8,128)S(1)}, f32[1,512]{1,0:T(1,128)S(1)}) custom-call(bf16[512,512]{1,0:T(8,128)(2,1)} %values_ref.1, s32[4,4]{1,0:T(4,128)} %tile_hbm.1, s32[4,4]{1,0:T(4,128)} %keep_hbm.1, s32[1,512]{1,0:T(1,128)} %bitcast.3), custom_call_target="tpu_custom_call" | custom-call | flops 4294967296 | bytes 2097152 | tf_op jit(solution)/shard_map/expand/pallas_call | solution.py:330
  62.6 0.9 %divide_convert_fusion = bf16[512,512]{1,0:T(8,128)(2,1)} fusion(f32[512,512]{1,0:T(8,128)S(1)} %get-tuple-element.7, f32[512]{0:T(512)S(1)} %bitcast.2), kind=kLoop, calls=%fused_computation | loop fusion | flops 524288 | bytes 1574912 | tf_op jit(solution)/shard_map/convert_element_type | solution.py:361
  (1 shorter events, 0.0 us)

commit v3 on v2

--- a/solution.py
+++ b/solution.py
@@ -17,7 +17,7 @@
 DEPTH = 8
 ORDER = BLOCK * GROUP
 AUG = 16
-ROUNDS = 4
+ROUNDS = 3
 MESH = pl.DeviceIdType.MESH
 
 UPPER, LOWER = (0, HALF), (HALF, HALF)
@@ -46,21 +46,42 @@
     ]
 
 
+SEAM = (192, 64)
+
+
 def depth_queue(step):
     first, second = (UPPER, LOWER) if step > 0 else (LOWER, UPPER)
+    last = ((0, 128), (128, 64)) if step > 0 else ((256, 128), (384, 128))
     return [
-        (0, first, 0, 2.1, 9.2),
-        (0, second, 0, 4.1, 9.2),
-        (-step, first, 2.1, 6.1, 9.2),
-        (-step, second, 4.1, 8.1, 9.2),
-        (-2 * step, first, 6.1, 10.1, 13.2),
-        (-2 * step, second, 8.1, 12.1, 13.2),
-        (-3 * step, quarter(first, 1), 10.1, 13.1, 15.2),
-        (-3 * step, quarter(first, -1), 10.1, 14.1, 15.2),
+        (0, first, 0, 2.1),
+        (0, second, 0, 4.1),
+        (-step, first, 2.1, 6.1),
+        (-step, second, 4.1, 8.1),
+        (-2 * step, first, 6.1, 10.1),
+        (-2 * step, second, 8.1, 12.1),
+        (-3 * step, last[0], 10.1, 13.1),
+        (-3 * step, last[1], 10.1, 14.1),
     ]
 
 
-STAGE_AFTER = {9.2: 0, 10.1: 1, 12.1: 2, 13.2: 3, 14.1: 4, 15: 5, 15.2: 6}
+def chip_queue():
+    moves = [(0, UPPER, 0, 9.2), (0, LOWER, 0, 9.2)]
+    for step in (1, -1):
+        first, second = (UPPER, LOWER) if step > 0 else (LOWER, UPPER)
+        moves += [
+            (-step, first, 2.1, 9.2),
+            (-step, second, 4.1, 9.2),
+            (-2 * step, first, 6.1, 9.2),
+            (-2 * step, second, 8.1, 9.2),
+            (-3 * step, first, 10.1, 14.2),
+            (-3 * step, second, 12.1, 14.2),
+            (-4 * step, quarter(first, 1), 13.1, 15.2),
+            (-4 * step, quarter(first, -1), 14.1, 15.2),
+        ]
+    return sorted(moves, key=lambda move: move[2])
+
+
+STAGE_AFTER = {10.1: (0, 1), 12.1: (2, 2), 13: (3, 3), 14.2: (4, 5)}
 
 
 def wrap(value, size):
@@ -70,7 +91,8 @@
 def kernel(
     values_ref, tile_hbm, keep_hbm, thr_hbm, pruned_ref, total_ref, tile_ref, keep_ref, thr_ref,
     rows_buf, cols_buf, acc, own, part_buf, sum_buf, tot_buf,
-    in_sem, send_sem, recv_sem, part_send, part_recv, sum_send, sum_recv, tot_send, tot_recv, ready_sem, round_sem,
+    in_sem, send_sem, recv_sem, part_send, part_recv, sum_send, sum_recv, tot_send, tot_recv, over_send, over_recv,
+    ready_sem, plane_sem, depth_sem,
 ):
     me_row, me_col = lax.axis_index("row"), lax.axis_index("col")
     x, y = lax.div(me_row, SIDE), lax.rem(me_row, SIDE)
@@ -114,7 +136,8 @@
     copies = []
 
     def copy_of(buf, slot, rows, number, target):
-        part = buf.at[slot, pl.ds(*rows), :]
+        above = AUG if buf is rows_buf else 0
+        part = buf.at[slot, pl.ds(rows[0] + above, rows[1]), :]
         return pltpu.make_async_remote_copy(
             src_ref=part, dst_ref=part, send_sem=send_sem.at[number], recv_sem=recv_sem.at[number],
             device_id=target, device_id_type=MESH,
@@ -139,71 +162,98 @@
                 )
         if place < 8:
             for step in (1, -1):
-                dz, rows, leaves, arrives, _ = depth_queue(step)[place]
+                dz, rows, leaves, arrives = depth_queue(step)[place]
                 add(
                     rows_buf, col_of(dz), col_of(dz - step), rows,
                     (me_row, col_of(step)), leaves, arrives, 4 + (step < 0),
                 )
-    for half in (UPPER, LOWER):
-        add(rows_buf, col_of(0), col_of(0, 1), half, partner, 0, 9.2)
-    for place in range(8):
-        for step in (1, -1):
-            dz, rows, _, arrives, other = depth_queue(step)[place]
-            add(rows_buf, col_of(dz - step), col_of(dz - step, 1), rows, partner, arrives, other)
-
-    def send(event, link=None):
-        for leaves, _, on, out, _ in copies:
-            if leaves == event and (event > 0 or on == link):
+    for dz, rows, leaves, arrives in chip_queue():
+        add(rows_buf, col_of(dz), col_of(dz, 1), rows, partner, leaves, arrives)
+
+    seam = len(copies)
+    seam_up = copy_of(rows_buf, col_of(-3), SEAM, seam, (me_row, col_of(1)))
+    seam_in = copy_of(rows_buf, col_of(4), SEAM, seam, (me_row, col_of(1)))
+    part = rows_buf.at[col_of(3), pl.ds(SEAM[0] + AUG, SEAM[1]), :]
+    seam_down = pltpu.make_async_remote_copy(
+        src_ref=part, dst_ref=part, send_sem=send_sem.at[seam + 1], recv_sem=recv_sem.at[seam],
+        device_id=(me_row, col_of(-1)), device_id_type=MESH,
+    )
+
+    def send(event, link=None, places=None):
+        for leaves, arrives, on, out, _ in copies:
+            if leaves == event and (event > 0 or on == link) and (places is None or arrives in places):
                 out.start()
+        if event == 10.1:
+
+            @pl.when(z < DEPTH - 1)
+            def _():
+                seam_up.start()
+
+        if event == 12.1:
+
+            @pl.when(z == 1)
+            def _():
+                seam_down.start()
 
     def receive(event):
         for _, arrives, _, _, into in copies:
             if arrives == event:
                 into.wait_recv()
-
-    def spread(number):
-        for neighbour in [partner] + [link[0] for link in links]:
-            pl.semaphore_signal(round_sem.at[number], inc=1, device_id=neighbour, device_id_type=MESH)
-        pl.semaphore_wait(round_sem.at[number], len(links) + 1)
+        if event == 14.1:
+            seam_in.wait_recv()
+
+    def spread(sem, number, neighbours):
+        for neighbour in neighbours:
+            pl.semaphore_signal(sem.at[number], inc=1, device_id=neighbour, device_id_type=MESH)
+        pl.semaphore_wait(sem.at[number], len(neighbours))
+
+    def spread_depth(number):
+        spread(depth_sem, number, [link[0] for link in links[4:]])
 
     def share(buf, sends, recvs, along_row):
-        def out(i):
-            if along_row:
-                target, slot = (lax.rem(me_row + i, GROUP), me_col), me_row
-            else:
-                target, slot = (me_row, lax.rem(me_col + i, GROUP)), me_col
+        count = GROUP if along_row else DEPTH
+
+        def slot_of(i):
+            return lax.rem(me_row + i, GROUP) if along_row else wrap(z + i, DEPTH) * 2 + core
+
+        def copy(i, slot):
+            target = (slot_of(i), me_col) if along_row else (me_row, slot_of(i))
             return pltpu.make_async_remote_copy(
                 src_ref=buf.at[slot], dst_ref=buf.at[slot], send_sem=sends.at[i], recv_sem=recvs.at[i],
                 device_id=target, device_id_type=MESH,
             )
 
-        def into(i):
-            if along_row:
-                target, slot = (lax.rem(me_row + i, GROUP), me_col), lax.rem(me_row + GROUP - i, GROUP)
-            else:
-                target, slot = (me_row, lax.rem(me_col + i, GROUP)), lax.rem(me_col + GROUP - i, GROUP)
-            return pltpu.make_async_remote_copy(
-                src_ref=buf.at[slot], dst_ref=buf.at[slot], send_sem=sends.at[i], recv_sem=recvs.at[i],
-                device_id=target, device_id_type=MESH,
-            )
-
         def start(i, carry):
-            out(i).start()
+            copy(i, slot_of(0)).start()
             return carry
 
         def arrive(i, carry):
-            into(i).wait_recv()
+            copy(i, slot_of(count - i)).wait_recv()
             return carry
 
         def finish(i, carry):
-            out(i).wait_send()
+            copy(i, slot_of(0)).wait_send()
             return carry
 
-        return tuple(functools.partial(lax.fori_loop, 1, GROUP, f, 0) for f in (start, arrive, finish))
+        return tuple(functools.partial(lax.fori_loop, 1, count, f, 0) for f in (start, arrive, finish))
 
     part_start, part_arrive, part_finish = share(part_buf, part_send, part_recv, True)
     sum_start, sum_arrive, sum_finish = share(sum_buf, sum_send, sum_recv, False)
     tot_start, tot_arrive, tot_finish = share(tot_buf, tot_send, tot_recv, True)
+
+    def over(i, other):
+        slot = wrap(z + i, DEPTH) * 2 + (1 - core if other else core)
+        return pltpu.make_async_remote_copy(
+            src_ref=sum_buf.at[slot], dst_ref=sum_buf.at[slot], send_sem=over_send.at[i], recv_sem=over_recv.at[i],
+            device_id=partner, device_id_type=MESH,
+        )
+
+    def over_all(act):
+        def one(i, carry):
+            act(i)
+            return carry
+
+        lax.fori_loop(0, DEPTH, one, 0)
 
     pl.semaphore_wait(barrier, lower)
     for number, (neighbour, theirs, mine) in enumerate(links):
@@ -221,25 +271,40 @@
             rows = slice(i * TB, (i + 1) * TB)
             tile = own[rows, cols].astype(jnp.float32) * tile_ref[i, j].astype(jnp.float32)
             part += jnp.sum(tile, axis=0, keepdims=True)
-            rows_buf[me_col, rows, cols] = tile.astype(jnp.bfloat16)
+            rows_buf[me_col, AUG + i * TB : AUG + (i + 1) * TB, cols] = tile.astype(jnp.bfloat16)
             cols_buf[me_row, rows, cols] = tile.astype(jnp.bfloat16)
         part_buf[me_row, :, cols] = part
     acc[...] = jnp.zeros_like(acc)
 
+    def early(number):
+        _, theirs, mine = links[number]
+
+        @pl.when(theirs < mine)
+        def _():
+            send(0, number, (2,) if number < 4 else None)
+
+    def late(number):
+        _, theirs, mine = links[number]
+
+        @pl.when(theirs > mine)
+        def _():
+            pl.semaphore_wait(ready_sem.at[number], 1)
+            send(0, number, (2,) if number < 4 else None)
+
+    for number in (4, 5, 0, 1, 2, 3):
+        early(number)
     send(0)
-    for number, (_, theirs, mine) in enumerate(links):
-
-        @pl.when(theirs > mine)
-        def _(number=number):
-            pl.semaphore_wait(ready_sem.at[number], 1)
-
-        send(0, number)
-
-    for number in range(ROUNDS - 1):
-        spread(number)
+    for number in range(5):
+        late(number)
+    for number in range(ROUNDS):
+        spread(plane_sem, number, [link[0] for link in links[:4]])
     part_start()
-
-    def multiply(stage):
+    for number in range(4):
+        send(0, number, (4,))
+    late(5)
+    spread_depth(0)
+
+    def multiply(low, high):
         def one(k, carry):
             dx = wrap(lax.div(k, SIDE) - x, SIDE)
             dy = wrap(lax.rem(k, SIDE) - y, SIDE)
@@ -253,11 +318,13 @@
 
             n, both = far(dx) + far(dy), off(dx) * off(dy)
             slow = lax.rem(k + core, 2)
-            by_plane = n * (2 - n) * (1 - both + both * lax.div(11 - dx - dy, 2)) + 5 * lax.div(n * (n - 1), 2)
+            by_plane = n * (2 - n) * (1 - both + both * lax.div(11 - dx - dy, 2)) + 6 * lax.div(n * (n - 1), 2)
             reach = dz * (DEPTH - dz)
-            by_depth = lax.div(reach, 15) * (2 + slow) + lax.div(reach, 16) * (2 + slow)
-
-            @pl.when(jnp.maximum(by_plane, by_depth) == stage)
+            by_depth = lax.div(reach, 15) * (2 + 2 * slow) + 3 * lax.div(reach, 16)
+
+            ready = jnp.maximum(by_plane, by_depth)
+
+            @pl.when((ready >= low) & (ready <= high))
             def _():
                 acc[...] += jnp.dot(rows_buf[k], cols_buf[k], preferred_element_type=jnp.float32)
 
@@ -268,9 +335,11 @@
     for event in sorted({arrives for _, arrives, *_ in copies}):
         receive(event)
         send(event)
+        if event == 2:
+            spread_depth(1)
         if event == 2.1:
-            spread(ROUNDS - 1)
-        if event == 4.1:
+            spread_depth(2)
+        if event == 4:
             part_arrive()
             sums = part_buf[0]
             for i in range(1, GROUP):
@@ -278,8 +347,11 @@
             sum_buf[me_col] = sums
             part_finish()
             sum_start()
+        if event == 8.1:
+            sum_arrive()
+            over_all(lambda i: over(i, 0).start())
         if event == 9.2:
-            sum_arrive()
+            over_all(lambda i: over(i, 1).wait_recv())
 
             def augment(k, carry):
                 s = sum_buf[k]
@@ -289,28 +361,56 @@
                 low = rest - mid
                 index = lax.broadcasted_iota(jnp.int32, (AUG, BLOCK), 0)
                 rows = jnp.where(index == 0, high, jnp.where(index == 1, mid, jnp.where(index == 2, low, 0.0)))
-                rows_buf[k, BLOCK:, :] = rows.astype(jnp.bfloat16)
+                rows_buf[k, :AUG, :] = rows.astype(jnp.bfloat16)
                 return carry
 
             lax.fori_loop(0, GROUP, augment, 0)
         if event in STAGE_AFTER:
-            multiply(STAGE_AFTER[event])
-
-    means = (acc[BLOCK : BLOCK + 1, :] + acc[BLOCK + 1 : BLOCK + 2, :] + acc[BLOCK + 2 : BLOCK + 3, :]) / ORDER
-    cut = 0.125 * thr_ref[...].astype(jnp.float32) * means
-    for j in range(TILES):
-        cols = slice(j * TB, (j + 1) * TB)
-        part = jnp.zeros((1, TB), jnp.float32)
-        for i in range(TILES):
-            rows = slice(i * TB, (i + 1) * TB)
-            tile = jnp.maximum(acc[rows, cols] - cut[:, cols], 0.0) * keep_ref[i, j].astype(jnp.float32)
-            pruned_ref[rows, cols] = tile
-            part += jnp.sum(tile, axis=0, keepdims=True)
-        tot_buf[me_row, :, cols] = part
+            multiply(*STAGE_AFTER[event])
+
+    def product(k):
+        return jnp.dot(rows_buf[k], cols_buf[k], preferred_element_type=jnp.float32)
+
+    def finish(last):
+        total = acc[...] + last
+        means = (total[0:1] + total[1:2] + total[2:3]) / ORDER
+        cut = 0.125 * thr_ref[...].astype(jnp.float32) * means
+        for j in range(TILES):
+            cols = slice(j * TB, (j + 1) * TB)
+            part = jnp.zeros((1, TB), jnp.float32)
+            for i in range(TILES):
+                tile = total[AUG + i * TB : AUG + (i + 1) * TB, cols]
+                tile = jnp.maximum(tile - cut[:, cols], 0.0) * keep_ref[i, j].astype(jnp.float32)
+                pruned_ref[i * TB : (i + 1) * TB, cols] = tile
+                part += jnp.sum(tile, axis=0, keepdims=True)
+            tot_buf[me_row, :, cols] = part
+
+    far_col, far_row = row_of(2, 2), col_of(4, 1)
+
+    @pl.when(far_col != far_row)
+    def _():
+        acc[...] += product(far_col) + product(far_row)
+
+    @pl.when(far_col == far_row)
+    def _():
+        acc[...] += product(far_col)
+
+    finish(0.0)
+
     sum_finish()
     tot_start()
     for _, _, _, out, _ in copies:
         out.wait_send()
+    over_all(lambda i: over(i, 0).wait_send())
+
+    @pl.when(z < DEPTH - 1)
+    def _():
+        seam_up.wait_send()
+
+    @pl.when(z == 1)
+    def _():
+        seam_down.wait_send()
+
     tot_arrive()
     totals = tot_buf[0]
     for i in range(1, GROUP):
@@ -320,7 +420,7 @@
 
 
 def n_copies():
-    return 40 + 16 + 2 + 16
+    return 40 + 16 + 18 + 2
 
 
 def on_device(values, tile_mask, keep_mask, thr_index):
@@ -347,8 +447,9 @@
             pltpu.VMEM((GROUP, 1, BLOCK), jnp.float32),
             pltpu.VMEM((GROUP, 1, BLOCK), jnp.float32),
             dma((4,)), dma((n_copies(),)), dma((n_copies(),)),
-            dma((GROUP,)), dma((GROUP,)), dma((GROUP,)), dma((GROUP,)), dma((GROUP,)), dma((GROUP,)),
-            pltpu.SemaphoreType.REGULAR((6,)), pltpu.SemaphoreType.REGULAR((ROUNDS,)),
+            dma((GROUP,)), dma((GROUP,)), dma((DEPTH,)), dma((DEPTH,)), dma((GROUP,)), dma((GROUP,)),
+            dma((DEPTH,)), dma((DEPTH,)),
+            pltpu.SemaphoreType.REGULAR((6,)), pltpu.SemaphoreType.REGULAR((ROUNDS,)), pltpu.SemaphoreType.REGULAR((ROUNDS,)),
         ],
         compiler_params=pltpu.CompilerParams(
             collective_id=0, has_side_effects=True, vmem_limit_bytes=40 * 1024 * 1024

time: 63.8 us -> 60 us (0.940)
  Pallas kernels: 62.6 us -> 58.8 us
    pallas_call x1, Pallas kernels: 62.6 us -> 58.8 us  [on_device(): pl.pallas_call(kernel, out_shape=(jax.ShapeDtypeStruct((BLOCK, BLOCK), jn...]
where the time goes in v3:
time: 60 us; the launch traced here: 59.8 us
  Pallas kernels  58.8 us (98%)
  other arithmetic  0.92 us (2%)
    pallas_call x1, Pallas kernels, on_device(): pl.pallas_call(kernel, out_shape=(jax.ShapeDtypeStruct((BLOCK, BLOCK), jn...  58.8 us

profile of v3, /device:TPU:8, one launch (start us, length us, event | category | flops | bytes accessed | tf_op | source)
XLA Modules:
  0.0 59.8 jit_solution(7522816110431998306)
XLA Ops:
  0.0 58.8 %expand.1 = (f32[512,512]{1,0:T(8,128)S(1)}, f32[1,512]{1,0:T(1,128)S(1)}) custom-call(bf16[512,512]{1,0:T(8,128)(2,1)} %values_ref.1, s32[4,4]{1,0:T(4,128)} %tile_hbm.1, s32[4,4]{1,0:T(4,128)} %keep_hbm.1, s32[1,512]{1,0:T(1,128)} %bitcast.3), custom_call_target="tpu_custom_call" | custom-call | flops 4294967296 | bytes 2097152 | tf_op jit(solution)/shard_map/expand/pallas_call | solution.py:430
  58.9 0.9 %divide_convert_fusion = bf16[512,512]{1,0:T(8,128)(2,1)} fusion(f32[512,512]{1,0:T(8,128)S(1)} %get-tuple-element.7, f32[512]{0:T(512)S(1)} %bitcast.2), kind=kLoop, calls=%fused_computation | loop fusion | flops 524288 | bytes 1574912 | tf_op jit(solution)/shard_map/convert_element_type | solution.py:462
  (1 shorter events, 0.0 us)

commit v4 on v3

--- a/solution.py
+++ b/solution.py
@@ -89,7 +89,7 @@
 
 
 def kernel(
-    values_ref, tile_hbm, keep_hbm, thr_hbm, pruned_ref, total_ref, tile_ref, keep_ref, thr_ref,
+    values_ref, tile_hbm, keep_hbm, thr_hbm, pruned_ref, scale_ref, tile_ref, keep_ref, thr_ref,
     rows_buf, cols_buf, acc, own, part_buf, sum_buf, tot_buf,
     in_sem, send_sem, recv_sem, part_send, part_recv, sum_send, sum_recv, tot_send, tot_recv, over_send, over_recv,
     ready_sem, plane_sem, depth_sem,
@@ -207,6 +207,9 @@
             pl.semaphore_signal(sem.at[number], inc=1, device_id=neighbour, device_id_type=MESH)
         pl.semaphore_wait(sem.at[number], len(neighbours))
 
+    def spread_plane(number):
+        spread(plane_sem, number, [link[0] for link in links[:4]])
+
     def spread_depth(number):
         spread(depth_sem, number, [link[0] for link in links[4:]])
 
@@ -237,7 +240,29 @@
 
         return tuple(functools.partial(lax.fori_loop, 1, count, f, 0) for f in (start, arrive, finish))
 
-    part_start, part_arrive, part_finish = share(part_buf, part_send, part_recv, True)
+
+    def part_copy(axis, d, slot):
+        number = axis * SIDE + d
+        return pltpu.make_async_remote_copy(
+            src_ref=part_buf.at[axis * SIDE + slot], dst_ref=part_buf.at[axis * SIDE + slot],
+            send_sem=part_send.at[number], recv_sem=part_recv.at[number],
+            device_id=(row_of(0, d) if axis else row_of(d, 0), me_col), device_id_type=MESH,
+        )
+
+    def part_start(axis):
+        for d in (2, 1, 3):
+            part_copy(axis, d, y if axis else x).start()
+
+    def part_finish(axis):
+        for d in range(1, SIDE):
+            part_copy(axis, d, y if axis else x).wait_send()
+
+    def part_total(axis):
+        for d in (1, 3, 2):
+            part_copy(axis, d, wrap((y if axis else x) - d, SIDE)).wait_recv()
+        slots = [part_buf[axis * SIDE + i] for i in range(SIDE)]
+        return (slots[0] + slots[1]) + (slots[2] + slots[3])
+
     sum_start, sum_arrive, sum_finish = share(sum_buf, sum_send, sum_recv, False)
     tot_start, tot_arrive, tot_finish = share(tot_buf, tot_send, tot_recv, True)
 
@@ -262,7 +287,8 @@
         def _(neighbour=neighbour, number=number):
             pl.semaphore_signal(ready_sem.at[number ^ 1], inc=1, device_id=neighbour, device_id_type=MESH)
 
-    for load in loads:
+    acc[...] = jnp.zeros_like(acc)
+    for load in loads[:2]:
         load.wait()
     for j in range(TILES):
         cols = slice(j * TB, (j + 1) * TB)
@@ -273,8 +299,10 @@
             part += jnp.sum(tile, axis=0, keepdims=True)
             rows_buf[me_col, AUG + i * TB : AUG + (i + 1) * TB, cols] = tile.astype(jnp.bfloat16)
             cols_buf[me_row, rows, cols] = tile.astype(jnp.bfloat16)
-        part_buf[me_row, :, cols] = part
-    acc[...] = jnp.zeros_like(acc)
+        part_buf[x, :, cols] = part
+
+    for load in loads[2:]:
+        load.wait()
 
     def early(number):
         _, theirs, mine = links[number]
@@ -296,9 +324,8 @@
     send(0)
     for number in range(5):
         late(number)
-    for number in range(ROUNDS):
-        spread(plane_sem, number, [link[0] for link in links[:4]])
-    part_start()
+    spread_plane(0)
+    part_start(0)
     for number in range(4):
         send(0, number, (4,))
     late(5)
@@ -334,23 +361,27 @@
 
     for event in sorted({arrives for _, arrives, *_ in copies}):
         receive(event)
+        if event == 2:
+            part_buf[SIDE + y] = part_total(0)
+            part_finish(0)
+            part_start(1)
         send(event)
         if event == 2:
             spread_depth(1)
         if event == 2.1:
             spread_depth(2)
         if event == 4:
-            part_arrive()
-            sums = part_buf[0]
-            for i in range(1, GROUP):
-                sums += part_buf[i]
-            sum_buf[me_col] = sums
-            part_finish()
+            spread_plane(1)
+        if event == 5:
+            sum_buf[me_col] = part_total(1)
+            part_finish(1)
             sum_start()
-        if event == 8.1:
+        if event == 7:
+            spread_plane(2)
+        if event == 9:
             sum_arrive()
             over_all(lambda i: over(i, 0).start())
-        if event == 9.2:
+        if event == 10.1:
             over_all(lambda i: over(i, 1).wait_recv())
 
             def augment(k, carry):
@@ -415,7 +446,7 @@
     totals = tot_buf[0]
     for i in range(1, GROUP):
         totals += tot_buf[i]
-    total_ref[...] = totals
+    scale_ref[...] = jnp.maximum(totals / ORDER, 0.1)
     tot_finish()
 
 
@@ -427,7 +458,7 @@
     vmem = pl.BlockSpec(memory_space=pltpu.VMEM)
     hbm = pl.BlockSpec(memory_space=pltpu.HBM)
     dma = pltpu.SemaphoreType.DMA
-    pruned, totals = pl.pallas_call(
+    pruned, scale = pl.pallas_call(
         kernel,
         out_shape=(
             jax.ShapeDtypeStruct((BLOCK, BLOCK), jnp.float32),
@@ -443,11 +474,11 @@
             pltpu.VMEM((GROUP, BLOCK, BLOCK), jnp.bfloat16),
             pltpu.VMEM((BLOCK + AUG, BLOCK), jnp.float32),
             pltpu.VMEM((BLOCK, BLOCK), jnp.bfloat16),
-            pltpu.VMEM((GROUP, 1, BLOCK), jnp.float32),
+            pltpu.VMEM((2 * SIDE, 1, BLOCK), jnp.float32),
             pltpu.VMEM((GROUP, 1, BLOCK), jnp.float32),
             pltpu.VMEM((GROUP, 1, BLOCK), jnp.float32),
             dma((4,)), dma((n_copies(),)), dma((n_copies(),)),
-            dma((GROUP,)), dma((GROUP,)), dma((DEPTH,)), dma((DEPTH,)), dma((GROUP,)), dma((GROUP,)),
+            dma((2 * SIDE,)), dma((2 * SIDE,)), dma((DEPTH,)), dma((DEPTH,)), dma((GROUP,)), dma((GROUP,)),
             dma((DEPTH,)), dma((DEPTH,)),
             pltpu.SemaphoreType.REGULAR((6,)), pltpu.SemaphoreType.REGULAR((ROUNDS,)), pltpu.SemaphoreType.REGULAR((ROUNDS,)),
         ],
@@ -459,7 +490,7 @@
         ),
         name="expand",
     )(*(pltpu.with_memory_space_constraint(a, pltpu.HBM) for a in (values, tile_mask, keep_mask, thr_index.reshape(1, BLOCK))))
-    return (pruned / jnp.maximum(totals / ORDER, 0.1)).astype(jnp.bfloat16)
+    return (pruned / scale).astype(jnp.bfloat16)
 
 
 def solution(mesh):

time: 60 us -> 59.7 us (level)
  no operation moved by 1% of the time
where the time goes in v4:
time: 59.7 us; the launch traced here: 59.6 us
  Pallas kernels  58.7 us (98%)
  other arithmetic  0.91 us (2%)
    pallas_call x1, Pallas kernels, on_device(): pl.pallas_call(kernel, out_shape=(jax.ShapeDtypeStruct((BLOCK, BLOCK), jn...  58.7 us

profile of v4, /device:TPU:8, one launch (start us, length us, event | category | flops | bytes accessed | tf_op | source)
XLA Modules:
  0.0 59.6 jit_solution(14253948377939072915)
XLA Ops:
  0.0 58.7 %expand.1 = (f32[512,512]{1,0:T(8,128)S(1)}, f32[1,512]{1,0:T(1,128)S(1)}) custom-call(bf16[512,512]{1,0:T(8,128)(2,1)} %values_ref.1, s32[4,4]{1,0:T(4,128)} %tile_hbm.1, s32[4,4]{1,0:T(4,128)} %keep_hbm.1, s32[1,512]{1,0:T(1,128)} %bitcast.3), custom_call_target="tpu_custom_call" | custom-call | flops 4294967296 | bytes 2097152 | tf_op jit(solution)/shard_map/expand/pallas_call | solution.py:461
  58.7 0.9 %divide_convert_fusion = bf16[512,512]{1,0:T(8,128)(2,1)} fusion(f32[512,512]{1,0:T(8,128)S(1)} %get-tuple-element.7, f32[512]{0:T(512)S(1)} %bitcast.2), kind=kLoop, calls=%fused_computation | loop fusion | flops 524288 | bytes 1574912 | tf_op jit(solution)/shard_map/convert_element_type | solution.py:493

commit v5 on v4

--- a/solution.py
+++ b/solution.py
@@ -59,8 +59,8 @@
         (-step, second, 4.1, 8.1),
         (-2 * step, first, 6.1, 10.1),
         (-2 * step, second, 8.1, 12.1),
-        (-3 * step, last[0], 10.1, 13.1),
-        (-3 * step, last[1], 10.1, 14.1),
+        (-3 * step, last[0], 10.1, 13.1 if step > 0 else 13.08),
+        (-3 * step, last[1], 10.1, 14.1 if step > 0 else 14.08),
     ]
 
 
@@ -75,13 +75,13 @@
             (-2 * step, second, 8.1, 9.2),
             (-3 * step, first, 10.1, 14.2),
             (-3 * step, second, 12.1, 14.2),
-            (-4 * step, quarter(first, 1), 13.1, 15.2),
-            (-4 * step, quarter(first, -1), 14.1, 15.2),
+            (-4 * step, quarter(first, 1), 13.1 if step > 0 else 13.08, 15.2),
+            (-4 * step, quarter(first, -1), 14.1 if step > 0 else 14.08, 15.2),
         ]
     return sorted(moves, key=lambda move: move[2])
 
 
-STAGE_AFTER = {10.1: (0, 1), 12.1: (2, 2), 13: (3, 3), 14.2: (4, 5)}
+STAGE_AFTER = {12.1: (2, 2), 13: (3, 3), 14.2: (4, 5)}
 
 
 def wrap(value, size):
@@ -396,6 +396,8 @@
                 return carry
 
             lax.fori_loop(0, GROUP, augment, 0)
+        if event in (10.1, 12):
+            pl.when(z > 0 if event == 10.1 else z == 0)(functools.partial(multiply, 0, 1))
         if event in STAGE_AFTER:
             multiply(*STAGE_AFTER[event])
 

time: 59.7 us -> 59.7 us (level)
  no operation moved by 1% of the time
where the time goes in v5:
time: 59.7 us; the launch traced here: 59.6 us
  Pallas kernels  58.7 us (98%)
  other arithmetic  0.91 us (2%)
    pallas_call x1, Pallas kernels, on_device(): pl.pallas_call(kernel, out_shape=(jax.ShapeDtypeStruct((BLOCK, BLOCK), jn...  58.7 us

profile of v5, /device:TPU:8, one launch (start us, length us, event | category | flops | bytes accessed | tf_op | source)
XLA Modules:
  0.0 59.6 jit_solution(2919116228513867102)
XLA Ops:
  0.0 58.7 %expand.1 = (f32[512,512]{1,0:T(8,128)S(1)}, f32[1,512]{1,0:T(1,128)S(1)}) custom-call(bf16[512,512]{1,0:T(8,128)(2,1)} %values_ref.1, s32[4,4]{1,0:T(4,128)} %tile_hbm.1, s32[4,4]{1,0:T(4,128)} %keep_hbm.1, s32[1,512]{1,0:T(1,128)} %bitcast.3), custom_call_target="tpu_custom_call" | custom-call | flops 4294967296 | bytes 2097152 | tf_op jit(solution)/shard_map/expand/pallas_call | solution.py:463
  58.7 0.9 %divide_convert_fusion = bf16[512,512]{1,0:T(8,128)(2,1)} fusion(f32[512,512]{1,0:T(8,128)S(1)} %get-tuple-element.7, f32[512]{0:T(512)S(1)} %bitcast.2), kind=kLoop, calls=%fused_computation | loop fusion | flops 524288 | bytes 1574912 | tf_op jit(solution)/shard_map/convert_element_type | solution.py:495

commit v6 on v5

--- a/solution.py
+++ b/solution.py
@@ -319,9 +319,8 @@
             pl.semaphore_wait(ready_sem.at[number], 1)
             send(0, number, (2,) if number < 4 else None)
 
-    for number in (4, 5, 0, 1, 2, 3):
+    for number in range(6):
         early(number)
-    send(0)
     for number in range(5):
         late(number)
     spread_plane(0)
@@ -329,6 +328,7 @@
     for number in range(4):
         send(0, number, (4,))
     late(5)
+    send(0)
     spread_depth(0)
 
     def multiply(low, high):

time: 59.7 us -> 59.7 us (level)
  no operation moved by 1% of the time
where the time goes in v6:
time: 59.7 us; the launch traced here: 59.6 us
  Pallas kernels  58.7 us (98%)
  other arithmetic  0.91 us (2%)
    pallas_call x1, Pallas kernels, on_device(): pl.pallas_call(kernel, out_shape=(jax.ShapeDtypeStruct((BLOCK, BLOCK), jn...  58.7 us

profile of v6, /device:TPU:8, one launch (start us, length us, event | category | flops | bytes accessed | tf_op | source)
XLA Modules:
  0.0 59.6 jit_solution(2761588234579478679)
XLA Ops:
  0.0 58.7 %expand.1 = (f32[512,512]{1,0:T(8,128)S(1)}, f32[1,512]{1,0:T(1,128)S(1)}) custom-call(bf16[512,512]{1,0:T(8,128)(2,1)} %values_ref.1, s32[4,4]{1,0:T(4,128)} %tile_hbm.1, s32[4,4]{1,0:T(4,128)} %keep_hbm.1, s32[1,512]{1,0:T(1,128)} %bitcast.3), custom_call_target="tpu_custom_call" | custom-call | flops 4294967296 | bytes 2097152 | tf_op jit(solution)/shard_map/expand/pallas_call | solution.py:463
  58.7 0.9 %divide_convert_fusion = bf16[512,512]{1,0:T(8,128)(2,1)} fusion(f32[512,512]{1,0:T(8,128)S(1)} %get-tuple-element.7, f32[512]{0:T(512)S(1)} %bitcast.2), kind=kLoop, calls=%fused_computation | loop fusion | flops 524288 | bytes 1574912 | tf_op jit(solution)/shard_map/convert_element_type | solution.py:495

commit v7 on v5

--- a/solution.py
+++ b/solution.py
@@ -264,7 +264,18 @@
         return (slots[0] + slots[1]) + (slots[2] + slots[3])
 
     sum_start, sum_arrive, sum_finish = share(sum_buf, sum_send, sum_recv, False)
-    tot_start, tot_arrive, tot_finish = share(tot_buf, tot_send, tot_recv, True)
+
+    def total_copy(dx, dy, slot):
+        return pltpu.make_async_remote_copy(
+            src_ref=tot_buf.at[slot], dst_ref=tot_buf.at[slot],
+            send_sem=tot_send.at[dx * SIDE + dy], recv_sem=tot_recv.at[dx * SIDE + dy],
+            device_id=(row_of(dx, dy), me_col), device_id_type=MESH,
+        )
+
+    apart = sorted(
+        ((dx, dy) for dx in range(SIDE) for dy in range(SIDE) if dx or dy),
+        key=lambda d: -sum(min(v, SIDE - v) for v in d),
+    )
 
     def over(i, other):
         slot = wrap(z + i, DEPTH) * 2 + (1 - core if other else core)
@@ -431,7 +442,8 @@
     finish(0.0)
 
     sum_finish()
-    tot_start()
+    for dx, dy in apart:
+        total_copy(dx, dy, me_row).start()
     for _, _, _, out, _ in copies:
         out.wait_send()
     over_all(lambda i: over(i, 0).wait_send())
@@ -444,12 +456,14 @@
     def _():
         seam_down.wait_send()
 
-    tot_arrive()
+    for dx, dy in apart:
+        total_copy(dx, dy, row_of(-dx, -dy)).wait_recv()
     totals = tot_buf[0]
     for i in range(1, GROUP):
         totals += tot_buf[i]
     scale_ref[...] = jnp.maximum(totals / ORDER, 0.1)
-    tot_finish()
+    for dx, dy in apart:
+        total_copy(dx, dy, me_row).wait_send()
 
 
 def n_copies():

time: 59.7 us -> 59.5 us (level)
  no operation moved by 1% of the time
where the time goes in v7:
time: 59.5 us; the launch traced here: 59.4 us
  Pallas kernels  58.5 us (98%)
  other arithmetic  0.91 us (2%)
    pallas_call x1, Pallas kernels, on_device(): pl.pallas_call(kernel, out_shape=(jax.ShapeDtypeStruct((BLOCK, BLOCK), jn...  58.5 us

profile of v7, /device:TPU:8, one launch (start us, length us, event | category | flops | bytes accessed | tf_op | source)
XLA Modules:
  0.0 59.4 jit_solution(15670872118820637950)
XLA Ops:
  0.0 58.5 %expand.1 = (f32[512,512]{1,0:T(8,128)S(1)}, f32[1,512]{1,0:T(1,128)S(1)}) custom-call(bf16[512,512]{1,0:T(8,128)(2,1)} %values_ref.1, s32[4,4]{1,0:T(4,128)} %tile_hbm.1, s32[4,4]{1,0:T(4,128)} %keep_hbm.1, s32[1,512]{1,0:T(1,128)} %bitcast.3), custom_call_target="tpu_custom_call" | custom-call | flops 4294967296 | bytes 2097152 | tf_op jit(solution)/shard_map/expand/pallas_call | solution.py:477
  58.5 0.9 %divide_convert_fusion = bf16[512,512]{1,0:T(8,128)(2,1)} fusion(f32[512,512]{1,0:T(8,128)S(1)} %get-tuple-element.7, f32[512]{0:T(512)S(1)} %bitcast.2), kind=kLoop, calls=%fused_computation | loop fusion | flops 524288 | bytes 1574912 | tf_op jit(solution)/shard_map/convert_element_type | solution.py:509
